TPU v7x, 32 devices: a whole 2x2x4 slice. The times are simulated.
32 devices in a mesh: section: 8 (over z, y), tensor: 4 (over x, core).
Axes of the slice: x: 2, y: 2, z: 4, core: 2. Of those that a mesh axis runs over, the one named last changes fastest.
Arguments:
- section_input: bfloat16 [8, 512, 4096], P('section', 'tensor'), may hold values from -6 to 6
- history: bfloat16 [8, 1, 512, 4096], P('section', None, 'tensor'), may hold values from -6 to 6
- query_weight: bfloat16 [8, 4096, 3072], P('section', None, 'tensor'), may hold values from -0.4 to 0.4
- key_weight: bfloat16 [8, 4096, 512], P('section', None, 'tensor'), may hold values from -0.4 to 0.4
- value_weight: bfloat16 [8, 4096, 512], P('section', None, 'tensor'), may hold values from -0.09375 to 0.09375
- output_weight: bfloat16 [8, 3072, 4096], P('section', 'tensor'), may hold values from -0.5 to 0.5
- mix_weights: float32 [8, 2], replicated, may hold values from 0.2 to 0.6
Outputs:
- next_input: bfloat16 [8, 512, 4096], P('section', 'tensor')
All inputs are finite; a program needn't handle non-finite values.
Results may differ from a plain program's by a relative error of at most 0.013.
The roundings to bfloat16 on the way count: a program that leaves them out, or rounds other values in their place, can miss the bound.
Values may be sent and summed in bfloat16 or wider, within the bound.
A program may use at most 128 MiB of HBM per device.

v0:
```python
import math

import jax
import jax.numpy as jnp
from jax import lax
from jax.sharding import PartitionSpec as P

HEAD_DIM = 64
DILATION_STRIDE = 4


def passed_along(value, axis, steps):
    count = lax.axis_size(axis)
    first, last = (max(0, -steps), min(count, count - steps))
    return lax.ppermute(value, axis, [(source, source + steps) for source in range(first, last)])


def from_behind(block, axis, distance):
    devices = range(lax.axis_size(axis))
    route = [((i - distance) % len(devices), i) for i in devices]
    return lax.ppermute(block, axis, route)


def normalize(token_rows):
    values = token_rows.astype(jnp.float32)
    inv_scale = lax.rsqrt(jnp.mean(values * values, axis=-1, keepdims=True) + 1e-05)
    return (values * inv_scale).astype(jnp.bfloat16)


def table_row(table, wanted):
    one_hot = (jnp.arange(table.shape[0], dtype=jnp.int32) == wanted).astype(jnp.float32)
    return jnp.sum(one_hot[:, None] * table, axis=0)


def attend(query_rows, key_rows, value_rows, first_row):
    scores = jnp.einsum(
        "tgjd,sgd->gjts", query_rows, key_rows, preferred_element_type=jnp.float32
    ) / math.sqrt(HEAD_DIM)
    row_positions = first_row + jnp.arange(query_rows.shape[0], dtype=jnp.int32)
    key_positions = jnp.arange(key_rows.shape[0], dtype=jnp.int32)
    scores = jnp.where(row_positions[:, None] >= key_positions[None, :], scores, -1e30)
    softmax_weights = jax.nn.softmax(scores, axis=-1).astype(jnp.bfloat16)
    heads_out = jnp.einsum(
        "gjts,sgd->tgjd", softmax_weights, value_rows, preferred_element_type=jnp.float32
    )
    return heads_out.astype(jnp.bfloat16)


def on_device(
    section_input, history, query_weight, key_weight, value_weight, output_weight, mix_weights
):
    token_rows = section_input[0]
    current_section = lax.axis_index("section")
    slots = history.shape[1]
    self_coefficient = table_row(mix_weights, current_section)
    history_sum = jnp.zeros(token_rows.shape, jnp.float32)
    for history_slot in range(1, slots + 1):
        received_block = passed_along(
            history[0, history_slot - 1], "section", DILATION_STRIDE * history_slot
        )
        factor = jnp.where(
            current_section >= DILATION_STRIDE * history_slot,
            self_coefficient[history_slot],
            jnp.float32(0.0),
        )
        history_sum = history_sum + factor * received_block.astype(jnp.float32)
    normed = normalize(token_rows)
    query_local = query_weight[0]
    key_local = key_weight[0]
    value_local = value_weight[0]
    row_piece = lax.all_gather(normed, "tensor", axis=0, tiled=True)
    query_part = jnp.dot(row_piece, query_local, preferred_element_type=jnp.float32).astype(
        jnp.bfloat16
    )
    key_part = jnp.dot(row_piece, key_local, preferred_element_type=jnp.float32).astype(
        jnp.bfloat16
    )
    value_part = jnp.dot(row_piece, value_local, preferred_element_type=jnp.float32).astype(
        jnp.bfloat16
    )
    projected = jnp.concatenate([query_part, key_part, value_part], axis=1)
    query_width = query_local.shape[1]
    kv_width = key_local.shape[1]
    seq_len = projected.shape[0]
    groups = kv_width // HEAD_DIM
    per_group = query_width // kv_width
    query_rows = projected[:, :query_width].reshape(seq_len, groups, per_group, HEAD_DIM)
    key_rows = projected[:, query_width : query_width + kv_width].reshape(seq_len, groups, HEAD_DIM)
    value_rows = projected[:, query_width + kv_width :].reshape(seq_len, groups, HEAD_DIM)
    block_rows = 512
    block_count = seq_len // block_rows
    blocked = query_rows.reshape(block_count, block_rows, groups, per_group, HEAD_DIM)
    starts = jnp.arange(block_count, dtype=jnp.int32) * block_rows
    attended = lax.map(
        lambda paired: attend(paired[0], key_rows, value_rows, paired[1]), (blocked, starts)
    )
    heads_out = attended.reshape(seq_len, query_width)
    output_local = output_weight[0]
    row_piece = heads_out
    partial_term = jnp.dot(row_piece, output_local, preferred_element_type=jnp.float32).astype(
        jnp.bfloat16
    )
    attention_sum = lax.psum_scatter(
        lax.optimization_barrier(partial_term).astype(jnp.float32).astype(jnp.bfloat16),
        "tensor",
        scatter_dimension=0,
        tiled=True,
    ).astype(jnp.float32)
    block_out = (token_rows.astype(jnp.float32) + attention_sum).astype(jnp.bfloat16)
    mixed = (self_coefficient[0] * block_out.astype(jnp.float32) + history_sum).astype(jnp.bfloat16)
    forwarded = from_behind(mixed, "section", 1)
    return forwarded[None]


def solution(mesh):
    placed = (
        P("section", "tensor", None),
        P("section", None, "tensor", None),
        P("section", None, "tensor"),
        P("section", None, "tensor"),
        P("section", None, "tensor"),
        P("section", "tensor", None),
        P(),
    )
    return jax.shard_map(
        on_device,
        mesh=mesh,
        in_specs=placed,
        out_specs=P("section", "tensor", None),
        check_vma=False,
    )
```

profile of v0, /device:TPU:0, one launch (start us, length us, event | category | flops | bytes accessed | tf_op | source)
XLA Modules:
  0.0 170.6 jit_solution(5231973395811371509)
XLA Ops:
  6.5 1.6 fusion.13
  8.2 2.5 %fusion.14 = bf16[128,4096]{1,0:T(8,128)(2,1)} fusion(bf16[1,128,4096]{2,1,0:T(8,128)(2,1)} %param.7, f32[128]{0:T(128)S(1)} %add_rsqrt_fusion), kind=kLoop, calls=%fused_computation.18 | loop fusion | flops 1572864 | bytes 2097664 | tf_op jit(solution)/shard_map/convert_element_type | solution.py:27
  10.6 0.0 all-gather.2.cloned.1.call-update
  10.6 0.0 reduce-scatter.2.cloned.1.call-start
  10.7 0.1 iota_compare_fusion
  10.8 37.2 %all-gather.2.cloned.1.call-done = bf16[512,4096]{1,0:T(8,128)(2,1)} async-done(((bf16[128,4096]{1,0:T(8,128)(2,1)}), bf16[512,4096]{1,0:T(8,128)(2,1)}) %all-gather.2.cloned.1.call-update) | async-done | bytes 4194320 | tf_op jit(solution)/shard_map/all_gather | solution.py:71
  48.0 7.5 %fusion.19 = bf16[512,768]{1,0:T(8,128)(2,1)S(1)} fusion(bf16[512,4096]{1,0:T(8,128)(2,1)} %all-gather.2.cloned.1.call-done, bf16[1,4096,768]{2,1,0:T(8,128)(2,1)} %param.9), kind=kOutput, calls=%fused_computation.23 | convolution fusion | flops 3221618688 | bytes 11272192 | tf_op jit(solution)/shard_map/dot_general | solution.py:72
  55.4 0.3 copy.10
  55.7 3.7 %convolution_convert_fusion = bf16[512,128]{0,1:T(8,128)(2,1)S(1)} fusion(bf16[512,4096]{1,0:T(8,128)(2,1)} %all-gather.2.cloned.1.call-done, bf16[1,4096,128]{2,1,0:T(8,128)(2,1)S(1)} %copy-done), kind=kOutput, calls=%fused_computation.24 | convolution fusion | flops 536936448 | bytes 5373952 | tf_op jit(solution)/shard_map/dot_general | solution.py:75
  59.5 7.3 %fusion.27 = (f32[2,6,512]{2,1,0:T(8,128)S(1)}, f32[2,6,512,512]{2,3,1,0:T(8,128)}) fusion(pred[512,512]{0,1:T(8,128)(4,1)S(1)} %iota_compare_fusion, bf16[512,2,64,1]{0,2,3,1:T(8,128)(2,1)S(1)} %bitcast.61, bf16[512,2,6,64]{0,3,2,1:T(8,128)(2,1)S(1)} %bitcast.60), kind=kOutput, calls=%fused_computation.35 | convolution fusion | flops 415236608 | bytes 13787136 | tf_op jit(solution)/shard_map/while/body/eval_jaxpr/sub | solution.py:42
  66.8 3.8 %convolution_convert_fusion.1 = bf16[512,128]{0,1:T(8,128)(2,1)S(1)} fusion(bf16[512,4096]{1,0:T(8,128)(2,1)} %all-gather.2.cloned.1.call-done, bf16[1,4096,128]{2,1,0:T(8,128)(2,1)S(1)} %copy-done.2), kind=kOutput, calls=%fused_computation.25 | convolution fusion | flops 536936448 | bytes 5373952 | tf_op jit(solution)/shard_map/dot_general | solution.py:78
  70.6 0.0 slice-start.1
  70.6 6.0 %fusion.18 = bf16[2,64,6,512]{3,1,2,0:T(8,128)(2,1)S(1)} fusion(bf16[512,2,64,1]{0,2,3,1:T(8,128)(2,1)S(1)} %bitcast.62, f32[2,6,512,512]{2,3,1,0:T(8,128)} %get-tuple-element.22, f32[2,6,512]{2,1,0:T(8,128)S(1)} %get-tuple-element.20), kind=kOutput, calls=%fused_computation.22 | convolution fusion | flops 409337856 | bytes 13524992 | tf_op jit(solution)/shard_map/while/body/eval_jaxpr/gjts,sgd->tgjd/dot_general | solution.py:43
  76.6 5.1 %fusion.10 = bf16[512,4096]{1,0:T(8,128)(2,1)} fusion(bf16[512,768]{0,1:T(8,128)(2,1)S(1)} %bitcast.66, bf16[1,768,4096]{2,1,0:T(8,128)(2,1)S(1)} %bitcast.64), kind=kOutput, calls=%fused_computation.13 | convolution fusion | flops 3223322624 | bytes 11272192 | tf_op jit(solution)/shard_map/dot_general | solution.py:100
  81.8 0.0 reduce-scatter.2.cloned.1.call-update
  81.8 4.5 %collective-permute-start = (bf16[128,4096]{1,0:T(8,128)(2,1)}, bf16[128,4096]{1,0:T(8,128)(2,1)S(1)}, u32[]{:S(2)}, u32[]{:S(2)}) collective-permute-start(bf16[128,4096]{1,0:T(8,128)(2,1)} %bitcast.65), channel_id=1, source_target_pairs={{0,16},{4,20},{8,24},{12,28},{1,17},{5,21},{9,25},{13,29},{2,18},{... | collective-permute-start | bytes 3145736 | tf_op jit(solution)/shard_map/ppermute | solution.py:15
  86.4 0.1 multiply_reduce_fusion
  86.5 0.6 fusion.26
  87.7 21.7 %collective-permute-done = bf16[128,4096]{1,0:T(8,128)(2,1)S(1)} collective-permute-done((bf16[128,4096]{1,0:T(8,128)(2,1)}, bf16[128,4096]{1,0:T(8,128)(2,1)S(1)}, u32[]{:S(2)}, u32[]{:S(2)}) %collective-permute-start) | collective-permute-done | bytes 1048608 | tf_op jit(solution)/shard_map/ppermute | solution.py:15
  109.4 17.1 %reduce-scatter.2.cloned.1.call-done = bf16[128,4096]{1,0:T(8,128)(2,1)} async-done(((bf16[512,4096]{1,0:T(8,128)(2,1)}), bf16[128,4096]{1,0:T(8,128)(2,1)}) %reduce-scatter.2.cloned.1.call-update) | async-done | bytes 1048592 | tf_op jit(solution)/shard_map/reduce_scatter | solution.py:103
  126.5 2.4 %add_convert_fusion = bf16[128,4096]{1,0:T(8,128)(2,1)S(1)} fusion(bf16[128,4096]{1,0:T(8,128)(2,1)S(1)} %collective-permute-done, bf16[128,4096]{1,0:T(8,128)(2,1)} %reduce-scatter.2.cloned.1.call-done, bf16[1,128,4096]{2,1,0:T(8,128)(2,1)S(1)} %copy-done.1, f32[]{:T(128)S(6)} %select_n.10, f32[]{:T(128)} %bitcast), kind=kLoop, calls=%fused_computation.20 | loop fusion | flops 5242880 | bytes 4194312 | tf_op jit(solution)/shard_map/convert_element_type | solution.py:110
  128.9 1.5 collective-permute-start.1
  130.4 32.3 %collective-permute-done.1 = bf16[128,4096]{1,0:T(8,128)(2,1)S(1)} collective-permute-done((bf16[128,4096]{1,0:T(8,128)(2,1)S(1)}, bf16[128,4096]{1,0:T(8,128)(2,1)S(1)}, u32[]{:S(2)}, u32[]{:S(2)}) %collective-permute-start.1) | collective-permute-done | bytes 1048608 | tf_op jit(solution)/shard_map/ppermute | solution.py:21
  162.8 1.0 copy.16
  (15 shorter events, 0.0 us)
Async XLA Ops:
  6.5 49.2 %copy-start = (bf16[1,4096,128]{2,1,0:T(8,128)(2,1)S(1)}, bf16[1,4096,128]{2,1,0:T(8,128)(2,1)}, u32[]{:S(2)}) copy-start(bf16[1,4096,128]{2,1,0:T(8,128)(2,1)} %param.10) | copy-start | bytes 3145732
  6.5 41.4 %all-gather.2.cloned.1.call-start = ((), (), s32[]{:S(2)}) async-start(), calls=%async_computation.1 | async-start | bytes 5242880 | tf_op jit(solution)/shard_map/all_gather | solution.py:71
  10.6 115.9 %reduce-scatter.2.cloned.1.call-start = ((), (), s32[]{:S(2)}) async-start(), calls=%async_computation.2 | async-start | bytes 5242880 | tf_op jit(solution)/shard_map/reduce_scatter | solution.py:103
  59.4 7.3 %copy-start.2 = (bf16[1,4096,128]{2,1,0:T(8,128)(2,1)S(1)}, bf16[1,4096,128]{2,1,0:T(8,128)(2,1)}, u32[]{:S(2)}) copy-start(bf16[1,4096,128]{2,1,0:T(8,128)(2,1)} %param.11) | copy-start | bytes 3145732
  66.8 9.9 %slice-start = ((s8[6291456]{0:T(1024)(128)(4,1)}), s8[4194304]{0:T(1024)(128)(4,1)S(1)}, s32[]{:S(2)}) async-start(s8[6291456]{0:T(1024)(128)(4,1)} %bitcast.63), calls=%async_computation.3 | async-start | bytes 8388608
  70.6 6.0 %slice-start.1 = ((s8[6291456]{0:T(1024)(128)(4,1)}), s8[2097152]{0:T(1024)(128)(4,1)S(1)}, s32[]{:S(2)}) async-start(s8[6291456]{0:T(1024)(128)(4,1)} %bitcast.63), calls=%async_computation.4 | async-start | bytes 4194304
  81.8 4.6 %copy-start.3 = (f32[8,2]{0,1:T(2,128)S(1)}, f32[8,2]{0,1:T(2,128)}, u32[]{:S(2)}) copy-start(f32[8,2]{0,1:T(2,128)} %param.13) | copy-start | bytes 196
  81.8 44.8 %copy-start.1 = (bf16[1,128,4096]{2,1,0:T(8,128)(2,1)S(1)}, bf16[1,128,4096]{2,1,0:T(8,128)(2,1)}, u32[]{:S(2)}) copy-start(bf16[1,128,4096]{2,1,0:T(8,128)(2,1)} %param.7) | copy-start | bytes 3145732
  81.8 27.6 %collective-permute-start = (bf16[128,4096]{1,0:T(8,128)(2,1)}, bf16[128,4096]{1,0:T(8,128)(2,1)S(1)}, u32[]{:S(2)}, u32[]{:S(2)}) collective-permute-start(bf16[128,4096]{1,0:T(8,128)(2,1)} %bitcast.65), channel_id=1, source_target_pairs={{0,16},{4,20},{8,24},{12,28},{1,17},{5,21},{9,25},{13,29},{2,18},{... | collective-permute-start | bytes 3145736 | tf_op jit(solution)/shard_map/ppermute | solution.py:15
  128.9 33.8 %collective-permute-start.1 = (bf16[128,4096]{1,0:T(8,128)(2,1)S(1)}, bf16[128,4096]{1,0:T(8,128)(2,1)S(1)}, u32[]{:S(2)}, u32[]{:S(2)}) collective-permute-start(bf16[128,4096]{1,0:T(8,128)(2,1)S(1)} %add_convert_fusion), channel_id=1, source_target_pairs={{28,0},{0,4},{4,8},{8,12},{12,16},{16,20},{20,24},{24,28},{29,1},{... | collective-permute-start | bytes 3145736 | tf_op jit(solution)/shard_map/ppermute | solution.py:21
Sparse Core Ops, SparseCore 0:
  10.8 37.1 all-gather.1
  81.9 44.5 reduce-scatter.1
where the time goes:
time: 171 us
  waiting for transfers between devices  108 us (63%)
  matrix products  33.4 us (20%)
  between operations  14.1 us (8%)
  other arithmetic  6.66 us (4%)
  starting transfers between devices  6.07 us (4%)
  local copies, waits for them, and re-layouts  1.89 us (1%)
    all_gather x1, waiting for transfers between devices, on_device(): row_piece = lax.all_gather(normed, 'tensor', axis=0, tiled=True)  37.2 us
    ppermute x1, waiting for transfers between devices, from_behind(): return lax.ppermute(block, axis, route)  32.3 us
    ppermute x1, waiting for transfers between devices, passed_along(): lax.ppermute(value, axis, [(source, source + steps) for source in range(f...  21.7 us
    reduce_scatter x1, waiting for transfers between devices, on_device(): lax.psum_scatter(lax.optimization_barrier(partial_term).astype(jnp.float3...  17.1 us
    dot_general x1, matrix products, on_device(): jnp.dot(row_piece, query_local, preferred_element_type=jnp.float32)  7.46 us
    sub x1, matrix products, attend(): softmax_weights = jax.nn.softmax(scores, axis=-1).astype(jnp.bfloat16)  7.3 us
    dot_general x1, matrix products, attend(): jnp.einsum('gjts,sgd->tgjd', softmax_weights, value_rows, preferred_eleme...  5.99 us
    dot_general x1, matrix products, on_device(): jnp.dot(row_piece, output_local, preferred_element_type=jnp.float32)  5.14 us
  transfers between devices with their start and end apart: 4, of which 4 were waited for; matrix products, arithmetic and copies ran while one was open for 0% of the time, Pallas kernels for 0%

commit v1 on v0

v1 whole, which is shorter than its diff:
```python
import functools
import math

import jax
import jax.numpy as jnp
from jax import lax
from jax.experimental import pallas as pl
from jax.experimental.pallas import tpu as pltpu
from jax.sharding import PartitionSpec as P

HEAD_DIM = 64
DILATION_STRIDE = 4
MESH = pl.DeviceIdType.MESH
LAG = 2


def start(copy):
    copy.start()
    return copy


def tick_kernel(
    sections,
    x_hbm,
    hist_hbm,
    wq_hbm,
    wk_hbm,
    wv_hbm,
    wo_hbm,
    mixw,
    out_hbm,
    x_own,
    chip_rows,
    peer_rows,
    w_all,
    w_out,
    q_all,
    k_pad,
    v_pad,
    heads,
    parts,
    sib_in,
    x_send,
    x_in,
    mixed,
    hist_in,
    w_sem,
    wo_sem,
    x_sem,
    hist_s,
    hist_r,
    sib_s,
    sib_r,
    gx_s,
    gx_r,
    fw_s,
    fw_r,
    rs_s,
    rs_r,
    xs_s,
    xs_r,
    out_s,
    out_r,
):
    section = lax.axis_index("section")
    me = lax.axis_index("tensor")
    hi, lo = me // 2, me % 2
    sibling = hi * 2 + (1 - lo)
    peer = (1 - hi) * 2 + lo
    rows, width = x_own.shape
    slots = hist_in.shape[0]
    chunks, both, _ = peer_rows.shape
    piece = both // 2
    q_tiles = w_all.shape[0] - 1
    tile = w_all.shape[2]
    half = tile // 2
    col_chunks, _, cols = w_out.shape
    nxt = lax.rem(section + 1, sections)
    prv = lax.rem(section + sections - 1, sections)

    load_x = start(pltpu.make_async_copy(x_hbm.at[0], x_own, x_sem))
    barrier = pltpu.get_barrier_semaphore()
    for other in (sibling, peer):
        pl.semaphore_signal(barrier, inc=1, device_id={"tensor": other}, device_id_type=MESH)
    for other in (nxt, prv):
        pl.semaphore_signal(barrier, inc=1, device_id={"section": other}, device_id_type=MESH)
    expected = jnp.int32(4)
    for k in range(1, slots + 1):
        step = DILATION_STRIDE * k
        forward, backward = section + step < sections, section >= step

        @pl.when(forward)
        def _():
            pl.semaphore_signal(
                barrier, inc=1, device_id={"section": section + step}, device_id_type=MESH
            )

        @pl.when(backward)
        def _():
            pl.semaphore_signal(
                barrier, inc=1, device_id={"section": section - step}, device_id_type=MESH
            )

        expected = expected + forward.astype(jnp.int32) + backward.astype(jnp.int32)

    loads = []
    for j in range(q_tiles):
        loads.append(
            pltpu.make_async_copy(
                wq_hbm.at[0, :, pl.ds(j * tile, tile)], w_all.at[j], w_sem.at[j]
            )
        )
    loads.append(
        pltpu.make_async_copy(
            wk_hbm.at[0], w_all.at[q_tiles, :, pl.ds(0, half)], w_sem.at[q_tiles]
        )
    )
    loads.append(
        pltpu.make_async_copy(
            wv_hbm.at[0], w_all.at[q_tiles, :, pl.ds(half, half)], w_sem.at[q_tiles + 1]
        )
    )
    load_x.wait()
    for copy in loads:
        copy.start()
    mine = pl.multiple_of(lo * rows, rows)

    def norm_rows(i, carry):
        at = pl.multiple_of(i * 16, 16)
        values = x_own[pl.ds(at, 16), :].astype(jnp.float32)
        inv = lax.rsqrt(jnp.mean(values * values, axis=-1, keepdims=True) + 1e-05)
        chip_rows[pl.ds(pl.multiple_of(mine + at, 16), 16), :] = (values * inv).astype(jnp.bfloat16)
        return carry

    lax.fori_loop(0, rows // 16, norm_rows, 0)
    pl.semaphore_wait(barrier, expected)

    def gather_copy(c):
        return pltpu.make_async_remote_copy(
            src_ref=chip_rows.at[pl.ds(pl.multiple_of(mine + c * piece, piece), piece)],
            dst_ref=peer_rows.at[c, pl.ds(pl.multiple_of(lo * piece, piece), piece)],
            send_sem=gx_s.at[c],
            recv_sem=gx_r.at[c],
            device_id={"tensor": peer},
            device_id_type=MESH,
        )

    def forward_copy(c):
        place = peer_rows.at[c, pl.ds(pl.multiple_of(lo * piece, piece), piece)]
        return pltpu.make_async_remote_copy(
            src_ref=place,
            dst_ref=place,
            send_sem=fw_s.at[c],
            recv_sem=fw_r.at[c],
            device_id={"tensor": sibling},
            device_id_type=MESH,
        )

    for c in range(chunks):
        gather_copy(c).start()
    own_place = chip_rows.at[pl.ds(mine, rows)]
    to_sibling = start(
        pltpu.make_async_remote_copy(
            src_ref=own_place,
            dst_ref=own_place,
            send_sem=sib_s,
            recv_sem=sib_r,
            device_id={"tensor": sibling},
            device_id_type=MESH,
        )
    )

    def hist_copy(k):
        return pltpu.make_async_remote_copy(
            src_ref=hist_hbm.at[0, k - 1],
            dst_ref=hist_in.at[k - 1],
            send_sem=hist_s.at[k - 1],
            recv_sem=hist_r.at[k - 1],
            device_id={"section": lax.rem(section + DILATION_STRIDE * k, sections)},
            device_id_type=MESH,
        )

    for k in range(1, slots + 1):
        step = DILATION_STRIDE * k

        @pl.when(section + step < sections)
        def _():
            hist_copy(k).start()

        @pl.when(section < step)
        def _():
            hist_in[k - 1] = jnp.zeros((rows, width), hist_in.dtype)

    out_loads = []
    for c in range(col_chunks):
        out_loads.append(
            start(
                pltpu.make_async_copy(
                    wo_hbm.at[0, :, pl.ds(c * cols, cols)], w_out.at[c], wo_sem.at[c]
                )
            )
        )

    scale = 1.0 / math.sqrt(HEAD_DIM)

    def project(rows_ref, spans):
        def q_tile(j, carry):
            acc = jnp.dot(rows_ref[...], w_all[j], preferred_element_type=jnp.float32)
            acc = (acc.astype(jnp.bfloat16) * jnp.bfloat16(scale)).astype(jnp.bfloat16)
            for source, target, size in spans:
                where = pl.ds(pl.multiple_of(target, size), size)
                q_all[2 * j, where, :] = acc[source : source + size, :half]
                q_all[2 * j + 1, where, :] = acc[source : source + size, half:]
            return carry

        lax.fori_loop(0, q_tiles, q_tile, 0)
        acc = jnp.dot(rows_ref[...], w_all[q_tiles], preferred_element_type=jnp.float32)
        acc = acc.astype(jnp.bfloat16).astype(jnp.float32)
        for part, padded in ((acc[:, :half], k_pad), (acc[:, half:], v_pad)):
            lane = lax.broadcasted_iota(jnp.int32, part.shape, 1)
            turned = pltpu.roll(part, HEAD_DIM, 1)
            low = lane < HEAD_DIM
            zero = jnp.zeros_like(part)
            forms = (
                jnp.where(low, part, zero),
                jnp.where(low, zero, turned),
                jnp.where(low, turned, zero),
                jnp.where(low, zero, part),
            )
            for f, form in enumerate(forms):
                form = form.astype(jnp.bfloat16)
                for source, target, size in spans:
                    where = pl.ds(pl.multiple_of(target, size), size)
                    padded[f, where, :] = form[source : source + size]

    for copy in loads:
        copy.wait()
    to_sibling.wait_recv()
    project(chip_rows, ((0, hi * 2 * rows, 2 * rows),))

    def peer_chunk(c, carry):
        gather_copy(c).wait_recv()
        forward_copy(c).start()
        forward_copy(c).wait_recv()
        base = (1 - hi) * 2 * rows + c * piece
        project(peer_rows.at[c], ((0, base, piece), (piece, base + rows, piece)))
        return carry

    lax.fori_loop(0, chunks, peer_chunk, 0)

    keys = k_pad.shape[1]
    pairs = q_all.shape[0]
    pairs_per_kv = pairs // (half // HEAD_DIM)

    def attend(side, first):
        def pair(p, carry):
            query = q_all[p, pl.ds(pl.multiple_of(first, 2 * rows), 2 * rows), :]
            row_at = first + lax.broadcasted_iota(jnp.int32, (2 * rows, keys), 0)
            key_at = lax.broadcasted_iota(jnp.int32, (2 * rows, keys), 1)
            seen = row_at >= key_at
            kv = p // pairs_per_kv
            total = None
            for which in range(2):
                scores = lax.dot_general(
                    query,
                    k_pad[kv * 2 + which],
                    (((1,), (1,)), ((), ())),
                    preferred_element_type=jnp.float32,
                )
                scores = jnp.where(seen, scores, -1e30)
                top = jnp.max(scores, axis=-1, keepdims=True)
                weights = jnp.exp(scores - top)
                weights = weights * (1.0 / jnp.sum(weights, axis=-1, keepdims=True))
                term = jnp.dot(
                    weights.astype(jnp.bfloat16),
                    v_pad[kv * 2 + which],
                    preferred_element_type=jnp.float32,
                )
                total = term if total is None else total + term
            heads[side, :, pl.ds(pl.multiple_of(p * half, half), half)] = total.astype(jnp.bfloat16)
            return carry

        lax.fori_loop(0, pairs, pair, 0)

    def sib_copy(side, c):
        return pltpu.make_async_remote_copy(
            src_ref=parts.at[side, c, 1 - lo],
            dst_ref=sib_in.at[side, c],
            send_sem=rs_s.at[side, c],
            recv_sem=rs_r.at[side, c],
            device_id={"tensor": sibling},
            device_id_type=MESH,
        )

    def peer_copy(c):
        return pltpu.make_async_remote_copy(
            src_ref=x_send.at[c],
            dst_ref=x_in.at[c],
            send_sem=xs_s.at[c],
            recv_sem=xs_r.at[c],
            device_id={"tensor": peer},
            device_id_type=MESH,
        )

    def out_copy(c):
        return pltpu.make_async_remote_copy(
            src_ref=mixed.at[c],
            dst_ref=out_hbm.at[0, :, pl.ds(pl.multiple_of(c * cols, cols), cols)],
            send_sem=out_s.at[c],
            recv_sem=out_r.at[c],
            device_id={"section": nxt},
            device_id_type=MESH,
        )

    def make_part(side, c):
        acc = jnp.dot(heads[side], w_out[c], preferred_element_type=jnp.float32)
        acc = acc.astype(jnp.bfloat16)
        parts[side, c, 0] = acc[:rows]
        parts[side, c, 1] = acc[rows:]
        sib_copy(side, c).start()

    def pair_sum(side, c):
        sib_copy(side, c).wait_recv()
        return parts[side, c, lo].astype(jnp.float32) + sib_in[side, c].astype(jnp.float32)

    attend(0, (1 - hi) * 2 * rows)
    for copy in out_loads:
        copy.wait()

    def peer_step(c, carry):
        @pl.when(c < col_chunks)
        def _():
            make_part(0, c)

        @pl.when(c >= LAG)
        def _():
            x_send[c - LAG] = pair_sum(0, c - LAG).astype(jnp.bfloat16)
            peer_copy(c - LAG).start()

        return carry

    lax.fori_loop(0, col_chunks + LAG, peer_step, 0)
    attend(1, hi * 2 * rows)

    def own_step(c, carry):
        make_part(1, c)
        return carry

    lax.fori_loop(0, col_chunks, own_step, 0)
    for k in range(1, slots + 1):

        @pl.when(section >= DILATION_STRIDE * k)
        def _():
            hist_copy(k).wait_recv()

    def final_step(c, carry):
        total = pair_sum(1, c)
        where = pl.ds(pl.multiple_of(c * cols, cols), cols)
        peer_copy(c).wait_recv()
        total = total + x_in[c].astype(jnp.float32)
        block = (x_own[:, where].astype(jnp.float32) + total).astype(jnp.bfloat16)
        value = mixw[section, 0] * block.astype(jnp.float32)
        for k in range(1, slots + 1):
            value = value + mixw[section, k] * hist_in[k - 1, :, where].astype(jnp.float32)
        mixed[c] = value.astype(jnp.bfloat16)
        out_copy(c).start()
        return carry

    lax.fori_loop(0, col_chunks, final_step, 0)

    to_sibling.wait_send()

    def drain_gather(c, carry):
        gather_copy(c).wait_send()
        forward_copy(c).wait_send()
        return carry

    lax.fori_loop(0, chunks, drain_gather, 0)
    for k in range(1, slots + 1):

        @pl.when(section + DILATION_STRIDE * k < sections)
        def _():
            hist_copy(k).wait_send()

    def drain(c, carry):
        sib_copy(0, c).wait_send()
        sib_copy(1, c).wait_send()
        peer_copy(c).wait_send()
        out_copy(c).wait()
        return carry

    lax.fori_loop(0, col_chunks, drain, 0)


def solution(mesh):
    sections, tensor = mesh.shape["section"], mesh.shape["tensor"]
    chunks, col_chunks = 2, 8

    def on_device(x, history, wq, wk, wv, wo, mix_weights):
        rows, width = x.shape[1:]
        slots = history.shape[1]
        q_width, kv_width = wq.shape[2], wk.shape[2]
        seq = rows * tensor
        tile = 2 * kv_width
        q_tiles = q_width // tile
        cols = width // col_chunks
        bf16 = jnp.bfloat16
        dma = pltpu.SemaphoreType.DMA
        hbm = pl.BlockSpec(memory_space=pl.ANY)
        piece = rows // chunks
        return pl.pallas_call(
            functools.partial(tick_kernel, sections),
            out_shape=jax.ShapeDtypeStruct(x.shape, bf16),
            in_specs=[hbm] * 6 + [pl.BlockSpec(memory_space=pltpu.SMEM)],
            out_specs=hbm,
            scratch_shapes=[
                pltpu.VMEM((rows, width), bf16),
                pltpu.VMEM((2 * rows, width), bf16),
                pltpu.VMEM((chunks, 2 * piece, width), bf16),
                pltpu.VMEM((q_tiles + 1, width, tile), bf16),
                pltpu.VMEM((col_chunks, q_width, cols), bf16),
                pltpu.VMEM((2 * q_tiles, seq, kv_width), bf16),
                pltpu.VMEM((4, seq, kv_width), bf16),
                pltpu.VMEM((4, seq, kv_width), bf16),
                pltpu.VMEM((2, 2 * rows, q_width), bf16),
                pltpu.VMEM((2, col_chunks, 2, rows, cols), bf16),
                pltpu.VMEM((2, col_chunks, rows, cols), bf16),
                pltpu.VMEM((col_chunks, rows, cols), bf16),
                pltpu.VMEM((col_chunks, rows, cols), bf16),
                pltpu.VMEM((col_chunks, rows, cols), bf16),
                pltpu.VMEM((slots, rows, width), bf16),
                dma((q_tiles + 2,)),
                dma((col_chunks,)),
                dma,
                dma((slots,)),
                dma((slots,)),
                dma,
                dma,
                dma((chunks,)),
                dma((chunks,)),
                dma((chunks,)),
                dma((chunks,)),
                dma((2, col_chunks)),
                dma((2, col_chunks)),
                dma((col_chunks,)),
                dma((col_chunks,)),
                dma((col_chunks,)),
                dma((col_chunks,)),
            ],
            compiler_params=pltpu.CompilerParams(
                collective_id=0, has_side_effects=True, vmem_limit_bytes=60 * 1024 * 1024
            ),
        )(x, history, wq, wk, wv, wo, mix_weights)

    placed = (
        P("section", "tensor", None),
        P("section", None, "tensor", None),
        P("section", None, "tensor"),
        P("section", None, "tensor"),
        P("section", None, "tensor"),
        P("section", "tensor", None),
        P(),
    )
    return jax.shard_map(
        on_device,
        mesh=mesh,
        in_specs=placed,
        out_specs=P("section", "tensor", None),
        check_vma=False,
    )
```

time: 171 us -> 83.4 us (0.49)
  waiting for transfers between devices: 108 us -> 0 us
  Pallas kernels: 0 us -> 79.5 us
  matrix products: 33.4 us -> 0 us
  between operations: 14.1 us -> 0.01 us
  other arithmetic: 6.66 us -> 0 us
  starting transfers between devices: 6.07 us -> 0 us
  local copies, waits for them, and re-layouts: 1.89 us -> 3.63 us
    pallas_call x0 -> x1, Pallas kernels: none -> 79.5 us  [on_device(): pl.pallas_call(functools.partial(tick_kernel, sections), out_shape=jax.Sh...]
    ppermute x2 -> x0, waiting for transfers between devices: 54 us -> none  [the longest x1 32.3 us: from_behind(): return lax.ppermute(block, axis, route)]
    all_gather x1 -> x0, waiting for transfers between devices: 37.2 us -> none  [on_device(): row_piece = lax.all_gather(normed, 'tensor', axis=0, tiled=True)]
    dot_general x5 -> x0, matrix products: 26.1 us -> none  [the longest x1 7.46 us: on_device(): jnp.dot(row_piece, query_local, preferred_element_type=jnp.float32)]
    reduce_scatter x1 -> x0, waiting for transfers between devices: 17.1 us -> none  [on_device(): lax.psum_scatter(lax.optimization_barrier(partial_term).astype(jnp.float3...]
    sub x1 -> x0, matrix products: 7.3 us -> none  [attend(): softmax_weights = jax.nn.softmax(scores, axis=-1).astype(jnp.bfloat16)]
    ppermute x2 -> x0, starting transfers between devices: 6.03 us -> none  [the longest x1 4.52 us: passed_along(): lax.ppermute(value, axis, [(source, source + steps) for source in range(f...]
    convert_element_type x3 -> x0, other arithmetic: 4.85 us -> none  [the longest x1 2.46 us: normalize(): return (values * inv_scale).astype(jnp.bfloat16)]
  transfers between devices with their start and end apart: 4 -> 0, of which waited for: 4 -> 0; matrix products, arithmetic and copies ran while one was open for 0% -> 0% of each run, Pallas kernels for 0% -> 0%
where the time goes in v1:
time: 83.4 us; the launch traced here: 83.2 us
  Pallas kernels  79.5 us (95%)
  local copies, waits for them, and re-layouts  3.63 us (4%)
    pallas_call x1, Pallas kernels, on_device(): pl.pallas_call(functools.partial(tick_kernel, sections), out_shape=jax.Sh...  79.5 us
    unnamed x2, local copies, waits for them, and re-layouts  3.63 us

profile of v1, /device:TPU:0, one launch (start us, length us, event | category | flops | bytes accessed | tf_op | source)
XLA Modules:
  0.0 83.2 jit_solution(5185276413568887039)
XLA Ops:
  0.0 1.3 %copy.8.mixw = f32[8,2]{1,0:T(8,128)} copy(f32[8,2]{0,1:T(2,128)} %param.13) | data formatting | bytes 128 | tf_op args[6]
  1.3 79.5 %shard_map.73 = bf16[1,128,4096]{2,1,0:T(8,128)(2,1)} custom-call(bf16[1,128,4096]{2,1,0:T(8,128)(2,1)} %x_hbm.1, bf16[1,1,128,4096]{3,2,1,0:T(8,128)(2,1)} %hist_hbm.1, bf16[1,4096,768]{2,1,0:T(8,128)(2,1)} %wq_hbm.1, bf16[1,4096,128]{2,1,0:T(8,128)(2,1)} %wk_hbm.1, bf16[1,4096,128]{2,1,0:T(8,128)(2,1)} %wv_hbm.1, bf16[1,768,4096]{2,1,0:T(8,128)(2,1)} %wo_hbm.1, ...), custom_call_target="tpu_custom_call" | custom-call | tf_op jit(solution)/shard_map/pallas_call | solution.py:411
  80.9 2.3 %copy.10 = bf16[1,128,4096]{2,1,0:T(8,128)(2,1)} copy(bf16[1,128,4096]{2,1,0:T(8,128)(2,1)} %shard_map.73) | data formatting | bytes 2097152

commit v2 on v1

v2 whole, which is shorter than its diff:
```python
import functools
import math

import jax
import jax.numpy as jnp
from jax import lax
from jax.experimental import pallas as pl
from jax.experimental.pallas import tpu as pltpu
from jax.sharding import PartitionSpec as P

HEAD_DIM = 64
DILATION_STRIDE = 4
MESH = pl.DeviceIdType.MESH
LAG = 2


def start(copy):
    copy.start()
    return copy


def tick_kernel(
    sections,
    x_hbm,
    hist_hbm,
    wq_hbm,
    wk_hbm,
    wv_hbm,
    wo_hbm,
    mix_hbm,
    out_hbm,
    x_own,
    chip_rows,
    peer_rows,
    w_all,
    w_out,
    q_all,
    k_pad,
    v_pad,
    peer_heads,
    own_heads,
    peer_keep,
    peer_give,
    peer_got,
    own_parts,
    own_got,
    x_in,
    mixed,
    hist_in,
    mix_v,
    w_sem,
    wo_sem,
    x_sem,
    mix_sem,
    hist_s,
    hist_r,
    sib_s,
    sib_r,
    gx_s,
    gx_r,
    fw_s,
    fw_r,
    ps_s,
    ps_r,
    os_s,
    os_r,
    xs_s,
    xs_r,
    out_s,
    out_r,
):
    section = lax.axis_index("section")
    me = lax.axis_index("tensor")
    hi, lo = me // 2, me % 2
    sibling = hi * 2 + (1 - lo)
    peer = (1 - hi) * 2 + lo
    rows, width = x_own.shape
    slots = hist_in.shape[0]
    piece = rows // 2
    q_tiles = w_all.shape[0] - 1
    tile = w_all.shape[2]
    half = tile // 2
    col_chunks, _, cols = w_out.shape
    side = col_chunks // 2
    nxt = lax.rem(section + 1, sections)
    prv = lax.rem(section + sections - 1, sections)

    load_x = start(pltpu.make_async_copy(x_hbm.at[0], x_own, x_sem))
    barrier = pltpu.get_barrier_semaphore()
    for other in (sibling, peer, (1 - hi) * 2 + (1 - lo)):
        pl.semaphore_signal(barrier, inc=1, device_id={"tensor": other}, device_id_type=MESH)
    for other in (nxt, prv):
        pl.semaphore_signal(barrier, inc=1, device_id={"section": other}, device_id_type=MESH)
    expected = jnp.int32(5)
    for k in range(1, slots + 1):
        step = DILATION_STRIDE * k
        forward, backward = section + step < sections, section >= step

        @pl.when(forward)
        def _():
            pl.semaphore_signal(
                barrier, inc=1, device_id={"section": section + step}, device_id_type=MESH
            )

        @pl.when(backward)
        def _():
            pl.semaphore_signal(
                barrier, inc=1, device_id={"section": section - step}, device_id_type=MESH
            )

        expected = expected + forward.astype(jnp.int32) + backward.astype(jnp.int32)

    loads = []
    for j in range(q_tiles):
        loads.append(
            pltpu.make_async_copy(
                wq_hbm.at[0, :, pl.ds(j * tile, tile)], w_all.at[j], w_sem.at[j]
            )
        )
    loads.append(
        pltpu.make_async_copy(
            wk_hbm.at[0], w_all.at[q_tiles, :, pl.ds(0, half)], w_sem.at[q_tiles]
        )
    )
    loads.append(
        pltpu.make_async_copy(
            wv_hbm.at[0], w_all.at[q_tiles, :, pl.ds(half, half)], w_sem.at[q_tiles + 1]
        )
    )
    load_x.wait()
    for copy in loads:
        copy.start()
    load_mix = start(pltpu.make_async_copy(mix_hbm, mix_v, mix_sem))
    mine = pl.multiple_of(lo * rows, rows)

    def norm_rows(i, carry):
        at = pl.multiple_of(i * 16, 16)
        values = x_own[pl.ds(at, 16), :].astype(jnp.float32)
        inv = lax.rsqrt(jnp.mean(values * values, axis=-1, keepdims=True) + 1e-05)
        chip_rows[pl.ds(pl.multiple_of(mine + at, 16), 16), :] = (values * inv).astype(jnp.bfloat16)
        return carry

    lax.fori_loop(0, rows // 16, norm_rows, 0)
    pl.semaphore_wait(barrier, expected)

    def gather_copy(j):
        return pltpu.make_async_remote_copy(
            src_ref=chip_rows.at[pl.ds(pl.multiple_of(j * rows + lo * piece, piece), piece)],
            dst_ref=peer_rows.at[j, pl.ds(pl.multiple_of(lo * piece, piece), piece)],
            send_sem=gx_s.at[j],
            recv_sem=gx_r.at[j],
            device_id={"tensor": peer},
            device_id_type=MESH,
        )

    def forward_copy(j):
        place = peer_rows.at[j, pl.ds(pl.multiple_of(lo * piece, piece), piece)]
        return pltpu.make_async_remote_copy(
            src_ref=place,
            dst_ref=place,
            send_sem=fw_s.at[j],
            recv_sem=fw_r.at[j],
            device_id={"tensor": sibling},
            device_id_type=MESH,
        )

    def sibling_copy(i):
        which = 1 - lo if i == 0 else lo
        place = chip_rows.at[pl.ds(pl.multiple_of(mine + which * piece, piece), piece)]
        return pltpu.make_async_remote_copy(
            src_ref=place,
            dst_ref=place,
            send_sem=sib_s.at[i],
            recv_sem=sib_r.at[i],
            device_id={"tensor": sibling},
            device_id_type=MESH,
        )

    @pl.when(lo == 0)
    def _():
        gather_copy(0).start()

    for i in range(2):
        sibling_copy(i).start()
    sibling_copy(0).wait_recv()

    @pl.when(lo == 1)
    def _():
        gather_copy(0).start()

    gather_copy(1).start()

    def hist_copy(k):
        return pltpu.make_async_remote_copy(
            src_ref=hist_hbm.at[0, k - 1],
            dst_ref=hist_in.at[k - 1],
            send_sem=hist_s.at[k - 1],
            recv_sem=hist_r.at[k - 1],
            device_id={"section": lax.rem(section + DILATION_STRIDE * k, sections)},
            device_id_type=MESH,
        )

    for k in range(1, slots + 1):
        step = DILATION_STRIDE * k

        @pl.when(section + step < sections)
        def _():
            hist_copy(k).start()

        @pl.when(section < step)
        def _():
            hist_in[k - 1] = jnp.zeros((rows, width), hist_in.dtype)

    out_loads = []
    for c in range(col_chunks):
        out_loads.append(
            start(
                pltpu.make_async_copy(
                    wo_hbm.at[0, :, pl.ds(c * cols, cols)], w_out.at[c], wo_sem.at[c]
                )
            )
        )

    scale = 1.0 / math.sqrt(HEAD_DIM)

    def project(rows_ref, target):
        size = rows_ref.shape[0]
        where = pl.ds(pl.multiple_of(target, size), size)

        def q_tile(j, carry):
            acc = jnp.dot(rows_ref[...], w_all[j], preferred_element_type=jnp.float32)
            acc = acc.astype(jnp.bfloat16) * jnp.bfloat16(scale)
            q_all[2 * j, where, :] = acc[:, :half]
            q_all[2 * j + 1, where, :] = acc[:, half:]
            return carry

        lax.fori_loop(0, q_tiles, q_tile, 0)
        acc = jnp.dot(rows_ref[...], w_all[q_tiles], preferred_element_type=jnp.float32)
        acc = acc.astype(jnp.bfloat16).astype(jnp.float32)
        for part, padded in ((acc[:, :half], k_pad), (acc[:, half:], v_pad)):
            lane = lax.broadcasted_iota(jnp.int32, part.shape, 1)
            turned = pltpu.roll(part, HEAD_DIM, 1)
            low = lane < HEAD_DIM
            zero = jnp.zeros_like(part)
            forms = (
                jnp.where(low, part, zero),
                jnp.where(low, zero, turned),
                jnp.where(low, turned, zero),
                jnp.where(low, zero, part),
            )
            for f, form in enumerate(forms):
                padded[f, where, :] = form.astype(jnp.bfloat16)

    pairs = q_all.shape[0]
    pairs_per_kv = pairs // (half // HEAD_DIM)

    def attend(heads_ref, first, size, keys):
        def pair(p, carry):
            query = q_all[p, first : first + size, :]
            row_at = first + lax.broadcasted_iota(jnp.int32, (size, keys), 0)
            key_at = lax.broadcasted_iota(jnp.int32, (size, keys), 1)
            seen = row_at >= key_at
            kv = p // pairs_per_kv
            total = None
            for which in range(2):
                scores = lax.dot_general(
                    query,
                    k_pad[kv * 2 + which, :keys, :],
                    (((1,), (1,)), ((), ())),
                    preferred_element_type=jnp.float32,
                )
                scores = jnp.where(seen, scores, -1e30)
                top = jnp.max(scores, axis=-1, keepdims=True)
                weights = jnp.exp(scores - top)
                weights = weights * (1.0 / jnp.sum(weights, axis=-1, keepdims=True))
                term = jnp.dot(
                    weights.astype(jnp.bfloat16),
                    v_pad[kv * 2 + which, :keys, :],
                    preferred_element_type=jnp.float32,
                )
                total = term if total is None else total + term
            heads_ref[:, pl.ds(pl.multiple_of(p * half, half), half)] = total.astype(jnp.bfloat16)
            return carry

        lax.fori_loop(0, pairs, pair, 0)

    def give_copy(j, i):
        return pltpu.make_async_remote_copy(
            src_ref=peer_give.at[j, i],
            dst_ref=peer_got.at[j, i],
            send_sem=ps_s.at[j, i],
            recv_sem=ps_r.at[j, i],
            device_id={"tensor": sibling},
            device_id_type=MESH,
        )

    def cross_copy(j, i):
        return pltpu.make_async_remote_copy(
            src_ref=peer_keep.at[j, i],
            dst_ref=x_in.at[lo * side + i],
            send_sem=xs_s.at[j, i],
            recv_sem=xs_r.at[lo * side + i],
            device_id={"tensor": (1 - hi) * 2 + j},
            device_id_type=MESH,
        )

    def cross_arrival(c):
        return pltpu.make_async_remote_copy(
            src_ref=x_in.at[c],
            dst_ref=x_in.at[c],
            send_sem=xs_s.at[0, 0],
            recv_sem=xs_r.at[c],
            device_id={"tensor": peer},
            device_id_type=MESH,
        )

    def peer_output(j):
        def part(c):
            acc = jnp.dot(peer_heads[j], w_out[c], preferred_element_type=jnp.float32)
            return acc.astype(jnp.bfloat16)

        def step(i, carry):
            @pl.when(i < side)
            def _():
                peer_give[j, i] = part((1 - lo) * side + i)
                peer_keep[j, i] = part(lo * side + i)
                give_copy(j, i).start()

            @pl.when(i >= LAG)
            def _():
                at = i - LAG
                give_copy(j, at).wait_recv()
                total = peer_keep[j, at].astype(jnp.float32) + peer_got[j, at].astype(jnp.float32)
                peer_keep[j, at] = total.astype(jnp.bfloat16)
                cross_copy(j, at).start()

            return carry

        lax.fori_loop(0, side + LAG, step, 0)

    def own_copy(c):
        return pltpu.make_async_remote_copy(
            src_ref=own_parts.at[c, 1 - lo],
            dst_ref=own_got.at[c],
            send_sem=os_s.at[c],
            recv_sem=os_r.at[c],
            device_id={"tensor": sibling},
            device_id_type=MESH,
        )

    def own_part(c):
        acc = jnp.dot(own_heads[...], w_out[c], preferred_element_type=jnp.float32)
        acc = acc.astype(jnp.bfloat16)
        own_parts[c, 0] = acc[:rows]
        own_parts[c, 1] = acc[rows:]
        own_copy(c).start()

    def out_copy(c):
        return pltpu.make_async_remote_copy(
            src_ref=mixed.at[c],
            dst_ref=out_hbm.at[0, :, pl.ds(pl.multiple_of(c * cols, cols), cols)],
            send_sem=out_s.at[c],
            recv_sem=out_r.at[c],
            device_id={"section": nxt},
            device_id_type=MESH,
        )

    for copy in loads:
        copy.wait()
    sibling_copy(1).wait_recv()
    project(chip_rows, hi * 2 * rows)
    for copy in out_loads:
        copy.wait()
    load_mix.wait()

    @pl.when(hi == 0)
    def _():
        attend(own_heads, 0, 2 * rows, 2 * rows)

        def own_step(c, carry):
            own_part(c)
            return carry

        lax.fori_loop(0, col_chunks, own_step, 0)

    for j in range(2):
        gather_copy(j).wait_recv()
        forward_copy(j).start()
        forward_copy(j).wait_recv()
        project(peer_rows.at[j], ((1 - hi) * 2 + j) * rows)

        @pl.when(hi == 0)
        def _():
            attend(peer_heads.at[j], (2 + j) * rows, rows, (3 + j) * rows)

        @pl.when(hi == 1)
        def _():
            attend(peer_heads.at[j], j * rows, rows, (1 + j) * rows)

        peer_output(j)

    @pl.when(hi == 1)
    def _():
        attend(own_heads, 2 * rows, 2 * rows, 4 * rows)

    for k in range(1, slots + 1):

        @pl.when(section >= DILATION_STRIDE * k)
        def _():
            hist_copy(k).wait_recv()

    def final_chunk(c):
        own_copy(c).wait_recv()
        total = own_parts[c, lo].astype(jnp.float32) + own_got[c].astype(jnp.float32)
        where = pl.ds(pl.multiple_of(c * cols, cols), cols)
        cross_arrival(c).wait_recv()
        total = total + x_in[c].astype(jnp.float32)
        block = (x_own[:, where].astype(jnp.float32) + total).astype(jnp.bfloat16)
        factors = mix_v[pl.ds(section, 1), :]
        value = factors[:, 0:1] * block.astype(jnp.float32)
        for k in range(1, slots + 1):
            past = hist_in[k - 1, :, where].astype(jnp.float32)
            value = value + factors[:, k : k + 1] * past
        mixed[c] = value.astype(jnp.bfloat16)
        out_copy(c).start()

    def column(i):
        return (i % 2) * side + i // 2

    def final_step(i, carry):
        @pl.when((i < col_chunks) & (hi == 1))
        def _():
            own_part(column(i))

        @pl.when(i >= LAG)
        def _():
            final_chunk(column(i - LAG))

        return carry

    lax.fori_loop(0, col_chunks + LAG, final_step, 0)

    for i in range(2):
        sibling_copy(i).wait_send()
        gather_copy(i).wait_send()
        forward_copy(i).wait_send()
    for k in range(1, slots + 1):

        @pl.when(section + DILATION_STRIDE * k < sections)
        def _():
            hist_copy(k).wait_send()

    def drain(c, carry):
        j, i = c // side, c % side
        give_copy(j, i).wait_send()
        cross_copy(j, i).wait_send()
        own_copy(c).wait_send()
        out_copy(c).wait()
        return carry

    lax.fori_loop(0, col_chunks, drain, 0)


def solution(mesh):
    sections, tensor = mesh.shape["section"], mesh.shape["tensor"]
    assert tensor == 4
    col_chunks = 8

    def on_device(x, history, wq, wk, wv, wo, mix_weights):
        rows, width = x.shape[1:]
        slots = history.shape[1]
        q_width, kv_width = wq.shape[2], wk.shape[2]
        seq = rows * tensor
        tile = 2 * kv_width
        q_tiles = q_width // tile
        cols = width // col_chunks
        bf16 = jnp.bfloat16
        dma = pltpu.SemaphoreType.DMA
        hbm = pl.BlockSpec(memory_space=pl.ANY)
        return pl.pallas_call(
            functools.partial(tick_kernel, sections),
            out_shape=jax.ShapeDtypeStruct(x.shape, bf16),
            in_specs=[hbm] * 7,
            out_specs=hbm,
            scratch_shapes=[
                pltpu.VMEM((rows, width), bf16),
                pltpu.VMEM((2 * rows, width), bf16),
                pltpu.VMEM((2, rows, width), bf16),
                pltpu.VMEM((q_tiles + 1, width, tile), bf16),
                pltpu.VMEM((col_chunks, q_width, cols), bf16),
                pltpu.VMEM((2 * q_tiles, seq, kv_width), bf16),
                pltpu.VMEM((4, seq, kv_width), bf16),
                pltpu.VMEM((4, seq, kv_width), bf16),
                pltpu.VMEM((2, rows, q_width), bf16),
                pltpu.VMEM((2 * rows, q_width), bf16),
                pltpu.VMEM((2, col_chunks // 2, rows, cols), bf16),
                pltpu.VMEM((2, col_chunks // 2, rows, cols), bf16),
                pltpu.VMEM((2, col_chunks // 2, rows, cols), bf16),
                pltpu.VMEM((col_chunks, 2, rows, cols), bf16),
                pltpu.VMEM((col_chunks, rows, cols), bf16),
                pltpu.VMEM((col_chunks, rows, cols), bf16),
                pltpu.VMEM((col_chunks, rows, cols), bf16),
                pltpu.VMEM((slots, rows, width), bf16),
                pltpu.VMEM(mix_weights.shape, mix_weights.dtype),
                dma((q_tiles + 2,)),
                dma((col_chunks,)),
                dma,
                dma,
                dma((slots,)),
                dma((slots,)),
                dma((2,)),
                dma((2,)),
                dma((2,)),
                dma((2,)),
                dma((2,)),
                dma((2,)),
                dma((2, col_chunks // 2)),
                dma((2, col_chunks // 2)),
                dma((col_chunks,)),
                dma((col_chunks,)),
                dma((2, col_chunks // 2)),
                dma((col_chunks,)),
                dma((col_chunks,)),
                dma((col_chunks,)),
            ],
            compiler_params=pltpu.CompilerParams(
                collective_id=0, has_side_effects=True, vmem_limit_bytes=60 * 1024 * 1024
            ),
        )(x, history, wq, wk, wv, wo, mix_weights)

    placed = (
        P("section", "tensor", None),
        P("section", None, "tensor", None),
        P("section", None, "tensor"),
        P("section", None, "tensor"),
        P("section", None, "tensor"),
        P("section", "tensor", None),
        P(),
    )
    return jax.shard_map(
        on_device,
        mesh=mesh,
        in_specs=placed,
        out_specs=P("section", "tensor", None),
        check_vma=False,
    )
```

time: 83.4 us -> 85.2 us (1.022)
  the two profiles are of different devices: /device:TPU:0 before, /device:TPU:3 now
where the time goes in v2:
time: 85.2 us; the launch traced here: 85 us
  Pallas kernels  81.3 us (95%)
  local copies, waits for them, and re-layouts  3.63 us (4%)
    pallas_call x1, Pallas kernels, on_device(): pl.pallas_call(functools.partial(tick_kernel, sections), out_shape=jax.Sh...  81.3 us
    unnamed x2, local copies, waits for them, and re-layouts  3.63 us

profile of v2, /device:TPU:3, one launch (start us, length us, event | category | flops | bytes accessed | tf_op | source)
XLA Modules:
  0.0 85.0 jit_solution(16977747819303259983)
XLA Ops:
  0.0 1.3 %copy.8.mix_hbm = f32[8,2]{1,0:T(8,128)} copy(f32[8,2]{0,1:T(2,128)} %param.13) | data formatting | bytes 128 | tf_op args[6]
  1.3 81.3 %shard_map.73 = bf16[1,128,4096]{2,1,0:T(8,128)(2,1)} custom-call(bf16[1,128,4096]{2,1,0:T(8,128)(2,1)} %x_hbm.1, bf16[1,1,128,4096]{3,2,1,0:T(8,128)(2,1)} %hist_hbm.1, bf16[1,4096,768]{2,1,0:T(8,128)(2,1)} %wq_hbm.1, bf16[1,4096,128]{2,1,0:T(8,128)(2,1)} %wk_hbm.1, bf16[1,4096,128]{2,1,0:T(8,128)(2,1)} %wv_hbm.1, bf16[1,768,4096]{2,1,0:T(8,128)(2,1)} %wo_hbm.1, ...), custom_call_target="tpu_custom_call" | custom-call | tf_op jit(solution)/shard_map/pallas_call | solution.py:480
  82.7 2.3 %copy.10 = bf16[1,128,4096]{2,1,0:T(8,128)(2,1)} copy(bf16[1,128,4096]{2,1,0:T(8,128)(2,1)} %shard_map.73) | data formatting | bytes 2097152

commit v3 on v2

--- a/solution.py
+++ b/solution.py
@@ -68,6 +68,8 @@
     xs_r,
     out_s,
     out_r,
+    block_in,
+    store_sem,
 ):
     section = lax.axis_index("section")
     me = lax.axis_index("tensor")
@@ -94,18 +96,21 @@
     expected = jnp.int32(5)
     for k in range(1, slots + 1):
         step = DILATION_STRIDE * k
-        forward, backward = section + step < sections, section >= step
+        forward, backward = section + step < sections, prv >= step
 
         @pl.when(forward)
         def _():
             pl.semaphore_signal(
-                barrier, inc=1, device_id={"section": section + step}, device_id_type=MESH
+                barrier,
+                inc=1,
+                device_id={"section": lax.rem(section + step + 1, sections)},
+                device_id_type=MESH,
             )
 
         @pl.when(backward)
         def _():
             pl.semaphore_signal(
-                barrier, inc=1, device_id={"section": section - step}, device_id_type=MESH
+                barrier, inc=1, device_id={"section": prv - step}, device_id_type=MESH
             )
 
         expected = expected + forward.astype(jnp.int32) + backward.astype(jnp.int32)
@@ -196,7 +201,7 @@
             dst_ref=hist_in.at[k - 1],
             send_sem=hist_s.at[k - 1],
             recv_sem=hist_r.at[k - 1],
-            device_id={"section": lax.rem(section + DILATION_STRIDE * k, sections)},
+            device_id={"section": lax.rem(section + DILATION_STRIDE * k + 1, sections)},
             device_id_type=MESH,
         )
 
@@ -207,7 +212,7 @@
         def _():
             hist_copy(k).start()
 
-        @pl.when(section < step)
+        @pl.when(prv < step)
         def _():
             hist_in[k - 1] = jnp.zeros((rows, width), hist_in.dtype)
 
@@ -358,7 +363,7 @@
     def out_copy(c):
         return pltpu.make_async_remote_copy(
             src_ref=mixed.at[c],
-            dst_ref=out_hbm.at[0, :, pl.ds(pl.multiple_of(c * cols, cols), cols)],
+            dst_ref=block_in.at[c],
             send_sem=out_s.at[c],
             recv_sem=out_r.at[c],
             device_id={"section": nxt},
@@ -403,12 +408,6 @@
     def _():
         attend(own_heads, 2 * rows, 2 * rows, 4 * rows)
 
-    for k in range(1, slots + 1):
-
-        @pl.when(section >= DILATION_STRIDE * k)
-        def _():
-            hist_copy(k).wait_recv()
-
     def final_chunk(c):
         own_copy(c).wait_recv()
         total = own_parts[c, lo].astype(jnp.float32) + own_got[c].astype(jnp.float32)
@@ -416,29 +415,52 @@
         cross_arrival(c).wait_recv()
         total = total + x_in[c].astype(jnp.float32)
         block = (x_own[:, where].astype(jnp.float32) + total).astype(jnp.bfloat16)
-        factors = mix_v[pl.ds(section, 1), :]
-        value = factors[:, 0:1] * block.astype(jnp.float32)
+        mixed[c] = block
+        out_copy(c).start()
+
+    def column(i):
+        return (i % 2) * side + i // 2
+
+    def final_step(i, carry):
+        @pl.when((i < col_chunks) & (hi == 1))
+        def _():
+            own_part(column(i))
+
+        @pl.when(i >= LAG)
+        def _():
+            final_chunk(column(i - LAG))
+
+        return carry
+
+    lax.fori_loop(0, col_chunks + LAG, final_step, 0)
+
+    for k in range(1, slots + 1):
+
+        @pl.when(prv >= DILATION_STRIDE * k)
+        def _():
+            hist_copy(k).wait_recv()
+
+    def store_copy(c):
+        return pltpu.make_async_copy(
+            block_in.at[c],
+            out_hbm.at[0, :, pl.ds(pl.multiple_of(c * cols, cols), cols)],
+            store_sem.at[c],
+        )
+
+    def mix_step(i, carry):
+        c = column(i)
+        out_copy(c).wait_recv()
+        where = pl.ds(pl.multiple_of(c * cols, cols), cols)
+        factors = mix_v[pl.ds(prv, 1), :]
+        value = factors[:, 0:1] * block_in[c].astype(jnp.float32)
         for k in range(1, slots + 1):
             past = hist_in[k - 1, :, where].astype(jnp.float32)
             value = value + factors[:, k : k + 1] * past
-        mixed[c] = value.astype(jnp.bfloat16)
-        out_copy(c).start()
-
-    def column(i):
-        return (i % 2) * side + i // 2
-
-    def final_step(i, carry):
-        @pl.when((i < col_chunks) & (hi == 1))
-        def _():
-            own_part(column(i))
-
-        @pl.when(i >= LAG)
-        def _():
-            final_chunk(column(i - LAG))
-
+        block_in[c] = value.astype(jnp.bfloat16)
+        store_copy(c).start()
         return carry
 
-    lax.fori_loop(0, col_chunks + LAG, final_step, 0)
+    lax.fori_loop(0, col_chunks, mix_step, 0)
 
     for i in range(2):
         sibling_copy(i).wait_send()
@@ -455,7 +477,8 @@
         give_copy(j, i).wait_send()
         cross_copy(j, i).wait_send()
         own_copy(c).wait_send()
-        out_copy(c).wait()
+        out_copy(c).wait_send()
+        store_copy(c).wait()
         return carry
 
     lax.fori_loop(0, col_chunks, drain, 0)
@@ -522,6 +545,8 @@
                 dma((col_chunks,)),
                 dma((col_chunks,)),
                 dma((col_chunks,)),
+                pltpu.VMEM((col_chunks, rows, cols), bf16),
+                dma((col_chunks,)),
             ],
             compiler_params=pltpu.CompilerParams(
                 collective_id=0, has_side_effects=True, vmem_limit_bytes=60 * 1024 * 1024

time: 85.2 us -> 79.8 us (0.937)
  the two profiles are of different devices: /device:TPU:3 before, /device:TPU:31 now
where the time goes in v3:
time: 79.8 us; the launch traced here: 79.6 us
  Pallas kernels  75.9 us (95%)
  local copies, waits for them, and re-layouts  3.63 us (5%)
    pallas_call x1, Pallas kernels, on_device(): pl.pallas_call(functools.partial(tick_kernel, sections), out_shape=jax.Sh...  75.9 us
    unnamed x2, local copies, waits for them, and re-layouts  3.63 us

profile of v3, /device:TPU:31, one launch (start us, length us, event | category | flops | bytes accessed | tf_op | source)
XLA Modules:
  0.0 79.6 jit_solution(4504320374905624678)
XLA Ops:
  0.0 1.3 %copy.8.mix_hbm = f32[8,2]{1,0:T(8,128)} copy(f32[8,2]{0,1:T(2,128)} %param.13) | data formatting | bytes 128 | tf_op args[6]
  1.3 75.9 %shard_map.73 = bf16[1,128,4096]{2,1,0:T(8,128)(2,1)} custom-call(bf16[1,128,4096]{2,1,0:T(8,128)(2,1)} %x_hbm.1, bf16[1,1,128,4096]{3,2,1,0:T(8,128)(2,1)} %hist_hbm.1, bf16[1,4096,768]{2,1,0:T(8,128)(2,1)} %wq_hbm.1, bf16[1,4096,128]{2,1,0:T(8,128)(2,1)} %wk_hbm.1, bf16[1,4096,128]{2,1,0:T(8,128)(2,1)} %wv_hbm.1, bf16[1,768,4096]{2,1,0:T(8,128)(2,1)} %wo_hbm.1, ...), custom_call_target="tpu_custom_call" | custom-call | tf_op jit(solution)/shard_map/pallas_call | solution.py:503
  77.3 2.3 %copy.10 = bf16[1,128,4096]{2,1,0:T(8,128)(2,1)} copy(bf16[1,128,4096]{2,1,0:T(8,128)(2,1)} %shard_map.73) | data formatting | bytes 2097152

commit v4 on v3

--- a/solution.py
+++ b/solution.py
@@ -228,7 +228,7 @@
 
     scale = 1.0 / math.sqrt(HEAD_DIM)
 
-    def project(rows_ref, target):
+    def project_query(rows_ref, target):
         size = rows_ref.shape[0]
         where = pl.ds(pl.multiple_of(target, size), size)
 
@@ -240,6 +240,10 @@
             return carry
 
         lax.fori_loop(0, q_tiles, q_tile, 0)
+
+    def project_key_value(rows_ref, target):
+        size = rows_ref.shape[0]
+        where = pl.ds(pl.multiple_of(target, size), size)
         acc = jnp.dot(rows_ref[...], w_all[q_tiles], preferred_element_type=jnp.float32)
         acc = acc.astype(jnp.bfloat16).astype(jnp.float32)
         for part, padded in ((acc[:, :half], k_pad), (acc[:, half:], v_pad)):
@@ -373,7 +377,8 @@
     for copy in loads:
         copy.wait()
     sibling_copy(1).wait_recv()
-    project(chip_rows, hi * 2 * rows)
+    project_key_value(chip_rows, hi * 2 * rows)
+    project_query(chip_rows, hi * 2 * rows)
     for copy in out_loads:
         copy.wait()
     load_mix.wait()
@@ -387,26 +392,6 @@
             return carry
 
         lax.fori_loop(0, col_chunks, own_step, 0)
-
-    for j in range(2):
-        gather_copy(j).wait_recv()
-        forward_copy(j).start()
-        forward_copy(j).wait_recv()
-        project(peer_rows.at[j], ((1 - hi) * 2 + j) * rows)
-
-        @pl.when(hi == 0)
-        def _():
-            attend(peer_heads.at[j], (2 + j) * rows, rows, (3 + j) * rows)
-
-        @pl.when(hi == 1)
-        def _():
-            attend(peer_heads.at[j], j * rows, rows, (1 + j) * rows)
-
-        peer_output(j)
-
-    @pl.when(hi == 1)
-    def _():
-        attend(own_heads, 2 * rows, 2 * rows, 4 * rows)
 
     def final_chunk(c):
         own_copy(c).wait_recv()
@@ -421,18 +406,59 @@
     def column(i):
         return (i % 2) * side + i // 2
 
-    def final_step(i, carry):
-        @pl.when((i < col_chunks) & (hi == 1))
-        def _():
+    def finish():
+        def final_step(i, carry):
+            final_chunk(column(i))
+            return carry
+
+        lax.fori_loop(0, col_chunks, final_step, 0)
+
+    def peer_queries(j):
+        project_query(peer_rows.at[j], ((1 - hi) * 2 + j) * rows)
+
+        @pl.when(hi == 0)
+        def _():
+            attend(peer_heads.at[j], (2 + j) * rows, rows, (3 + j) * rows)
+
+        @pl.when(hi == 1)
+        def _():
+            attend(peer_heads.at[j], j * rows, rows, (1 + j) * rows)
+
+        peer_output(j)
+
+    for j in range(2):
+        gather_copy(j).wait_recv()
+        forward_copy(j).start()
+        forward_copy(j).wait_recv()
+        project_key_value(peer_rows.at[j], ((1 - hi) * 2 + j) * rows)
+        if j == 0:
+            peer_queries(j)
+
+    @pl.when(hi == 1)
+    def _():
+        attend(own_heads, 2 * rows, 2 * rows, 4 * rows)
+
+        def own_step(i, carry):
             own_part(column(i))
 
-        @pl.when(i >= LAG)
-        def _():
-            final_chunk(column(i - LAG))
-
-        return carry
-
-    lax.fori_loop(0, col_chunks + LAG, final_step, 0)
+            @pl.when((lo == 0) & (i >= LAG))
+            def _():
+                final_chunk(column(i - LAG))
+
+            return carry
+
+        lax.fori_loop(0, col_chunks, own_step, 0)
+
+        @pl.when(lo == 0)
+        def _():
+            for i in range(col_chunks - LAG, col_chunks):
+                final_chunk(column(i))
+
+    peer_queries(1)
+
+    @pl.when((hi == 0) | (lo == 1))
+    def _():
+        finish()
 
     for k in range(1, slots + 1):
 

time: 79.8 us -> 79.7 us (level)
  no operation moved by 1% of the time
where the time goes in v4:
time: 79.7 us; the launch traced here: 79.5 us
  Pallas kernels  75.8 us (95%)
  local copies, waits for them, and re-layouts  3.63 us (5%)
    pallas_call x1, Pallas kernels, on_device(): pl.pallas_call(functools.partial(tick_kernel, sections), out_shape=jax.Sh...  75.8 us
    unnamed x2, local copies, waits for them, and re-layouts  3.63 us

profile of v4, /device:TPU:31, one launch (start us, length us, event | category | flops | bytes accessed | tf_op | source)
XLA Modules:
  0.0 79.5 jit_solution(6975621642893296844)
XLA Ops:
  0.0 1.3 %copy.8.mix_hbm = f32[8,2]{1,0:T(8,128)} copy(f32[8,2]{0,1:T(2,128)} %param.13) | data formatting | bytes 128 | tf_op args[6]
  1.3 75.8 %shard_map.73 = bf16[1,128,4096]{2,1,0:T(8,128)(2,1)} custom-call(bf16[1,128,4096]{2,1,0:T(8,128)(2,1)} %x_hbm.1, bf16[1,1,128,4096]{3,2,1,0:T(8,128)(2,1)} %hist_hbm.1, bf16[1,4096,768]{2,1,0:T(8,128)(2,1)} %wq_hbm.1, bf16[1,4096,128]{2,1,0:T(8,128)(2,1)} %wk_hbm.1, bf16[1,4096,128]{2,1,0:T(8,128)(2,1)} %wv_hbm.1, bf16[1,768,4096]{2,1,0:T(8,128)(2,1)} %wo_hbm.1, ...), custom_call_target="tpu_custom_call" | custom-call | tf_op jit(solution)/shard_map/pallas_call | solution.py:529
  77.2 2.3 %copy.10 = bf16[1,128,4096]{2,1,0:T(8,128)(2,1)} copy(bf16[1,128,4096]{2,1,0:T(8,128)(2,1)} %shard_map.73) | data formatting | bytes 2097152

commit v5 on v4

--- a/solution.py
+++ b/solution.py
@@ -424,6 +424,12 @@
         def _():
             attend(peer_heads.at[j], j * rows, rows, (1 + j) * rows)
 
+        if j == 1:
+
+            @pl.when((hi == 0) & (lo == 0))
+            def _():
+                finish()
+
         peer_output(j)
 
     for j in range(2):
@@ -456,7 +462,7 @@
 
     peer_queries(1)
 
-    @pl.when((hi == 0) | (lo == 1))
+    @pl.when(lo == 1)
     def _():
         finish()
 

time: 79.7 us -> 79.7 us (level)
  no operation moved by 1% of the time
where the time goes in v5:
time: 79.7 us; the launch traced here: 79.5 us
  Pallas kernels  75.8 us (95%)
  local copies, waits for them, and re-layouts  3.63 us (5%)
    pallas_call x1, Pallas kernels, on_device(): pl.pallas_call(functools.partial(tick_kernel, sections), out_shape=jax.Sh...  75.8 us
    unnamed x2, local copies, waits for them, and re-layouts  3.63 us

profile of v5, /device:TPU:31, one launch (start us, length us, event | category | flops | bytes accessed | tf_op | source)
XLA Modules:
  0.0 79.5 jit_solution(10956975017258019827)
XLA Ops:
  0.0 1.3 %copy.8.mix_hbm = f32[8,2]{1,0:T(8,128)} copy(f32[8,2]{0,1:T(2,128)} %param.13) | data formatting | bytes 128 | tf_op args[6]
  1.3 75.8 %shard_map.73 = bf16[1,128,4096]{2,1,0:T(8,128)(2,1)} custom-call(bf16[1,128,4096]{2,1,0:T(8,128)(2,1)} %x_hbm.1, bf16[1,1,128,4096]{3,2,1,0:T(8,128)(2,1)} %hist_hbm.1, bf16[1,4096,768]{2,1,0:T(8,128)(2,1)} %wq_hbm.1, bf16[1,4096,128]{2,1,0:T(8,128)(2,1)} %wk_hbm.1, bf16[1,4096,128]{2,1,0:T(8,128)(2,1)} %wv_hbm.1, bf16[1,768,4096]{2,1,0:T(8,128)(2,1)} %wo_hbm.1, ...), custom_call_target="tpu_custom_call" | custom-call | tf_op jit(solution)/shard_map/pallas_call | solution.py:535
  77.2 2.3 %copy.10 = bf16[1,128,4096]{2,1,0:T(8,128)(2,1)} copy(bf16[1,128,4096]{2,1,0:T(8,128)(2,1)} %shard_map.73) | data formatting | bytes 2097152
